TPU v7x, 32 devices: a whole 2x2x4 slice. The times are simulated.
32 devices in a mesh: seq: 8 (over y, x, core), head: 4 (over z).
Axes of the slice: x: 2, y: 2, z: 4, core: 2. Of those that a mesh axis runs over, the one named last changes fastest.
Arguments:
- text_states: bfloat16 [2048, 4096], P('seq', 'head'), may hold values from -200 to 200
- query_weight: bfloat16 [4096, 4096], P(None, 'head'), may hold values from -0.09375 to 0.09375
- image_keys: bfloat16 [4096, 1024], P('seq', 'head'), may hold values from -12 to 12
- image_values: bfloat16 [4096, 1024], P('seq', 'head'), may hold values from -24 to 24
- output_weight: bfloat16 [4096, 4096], P('head'), may hold values from -0.09375 to 0.09375
- attn_gate: float32 [1], replicated, may hold values from 0.3 to 1.5
- frame_lengths: int32 [16], replicated, may hold values from 1 to 512, 4096 in all
- frame_limit: int32 [32], replicated, may hold values from 0 to 16
Outputs:
- gated_branch: bfloat16 [2048, 4096], P('seq', 'head')
Inputs may be any that keep to these rules, and one draw needn't show every extreme that they name: `frame_lengths`: the lengths sum to 4096.
All inputs are finite; a program needn't handle non-finite values.
Results may differ from a plain program's by a relative error of at most 0.014.
The roundings to bfloat16 on the way count: a program that leaves them out, or rounds other values in their place, can miss the bound.
Values may be sent and summed in bfloat16 or wider, within the bound.
No kernel may reach another device: no remote copies, remote signals or barrier semaphores. Data moves between devices by JAX's collectives and lax.ppermute only.
A program may use at most 128 MiB of HBM per device.

v0:
```python
import math
import jax
import jax.numpy as jnp
from jax import lax
from jax.sharding import PartitionSpec as P

HD = 128
TBLK = 64
GROUP = 4
masked_fill = -1e30


def from_behind(block, axis, distance):
    devices = range(lax.axis_size(axis))
    route = [((i - distance) % len(devices), i) for i in devices]
    return lax.ppermute(block, axis, route)


def shards(
    text_states,
    query_weight,
    image_keys,
    image_values,
    output_weight,
    attn_gate,
    frame_lengths,
    frame_limit,
):
    text_rows = text_states.shape[0]
    video_rows = image_keys.shape[0]
    local_kv = image_keys.shape[1] // HD
    seq_index = lax.axis_index("seq")
    cycle_size = lax.axis_size("seq")
    score_scale = 1.0 / math.sqrt(HD)
    queries = jnp.dot(
        lax.all_gather(text_states, "head", axis=1, tiled=True),
        query_weight,
        preferred_element_type=jnp.float32,
    ).astype(jnp.bfloat16)
    grouped_queries = (
        queries.reshape(text_rows, local_kv, GROUP, HD)
        .transpose(1, 2, 0, 3)
        .reshape(local_kv, GROUP * text_rows, HD)
    )
    frame_ends = jnp.cumsum(frame_lengths)
    block_count = text_rows // TBLK
    my_limits = lax.dynamic_slice_in_dim(frame_limit, seq_index * block_count, block_count, 0)
    group_limits = jnp.tile(jnp.repeat(my_limits, TBLK), GROUP)

    def dense_block(running, key_block, value_block, key_frames):
        best_score, weight_sum, accumulated = running
        key_head_count = key_block.reshape(key_block.shape[0], local_kv, HD)
        value_heads = value_block.reshape(value_block.shape[0], local_kv, HD)
        scores = (
            jnp.einsum(
                "sxn,lsn->sxl", grouped_queries, key_head_count, preferred_element_type=jnp.float32
            )
            * score_scale
        )
        visible = key_frames[None, None, :] < group_limits[None, :, None]
        block_best = jnp.max(jnp.where(visible, scores, masked_fill), axis=2)
        new_best = jnp.maximum(best_score, block_best)
        weights = jnp.where(visible, jnp.exp(scores - new_best[:, :, None]), 0.0)
        factor = jnp.exp(best_score - new_best)
        weight_sum = weight_sum * factor + jnp.sum(weights, axis=2)
        mixed = jnp.einsum(
            "vus,svg->vug",
            weights.astype(jnp.bfloat16),
            value_heads,
            preferred_element_type=jnp.float32,
        )
        accumulated = accumulated * factor[:, :, None] + mixed
        return (new_best, weight_sum, accumulated)

    def attend_frames(running, key_block, value_block, first_row):
        token_positions = first_row + jnp.arange(key_block.shape[0], dtype=jnp.int32)
        key_frames = jnp.sum(
            (frame_ends[None, :] <= token_positions[:, None]).astype(jnp.int32), axis=1
        )
        return dense_block(running, key_block, value_block, key_frames)

    initial = (
        jnp.full((local_kv, GROUP * text_rows), masked_fill, jnp.float32),
        jnp.zeros((local_kv, GROUP * text_rows), jnp.float32),
        jnp.zeros((local_kv, GROUP * text_rows, HD), jnp.float32),
    )
    half_rows = video_rows // 2

    def paired_turn(turn_index, state_in):
        running, keys_up, values_up, keys_down, values_down = state_in
        source_up = (seq_index - turn_index) % cycle_size
        source_down = (seq_index + turn_index) % cycle_size
        running = attend_frames(running, keys_up, values_up, source_up * video_rows)
        running = attend_frames(
            running, keys_down, values_down, source_down * video_rows + half_rows
        )
        keys_up, values_up = from_behind((keys_up, values_up), "seq", 1)
        keys_down, values_down = from_behind((keys_down, values_down), "seq", -1)
        return (running, keys_up, values_up, keys_down, values_down)

    start_state = (
        initial,
        image_keys[:half_rows],
        image_values[:half_rows],
        image_keys[half_rows:],
        image_values[half_rows:],
    )
    running, keys_up, values_up, keys_down, values_down = lax.fori_loop(
        0, cycle_size - 1, paired_turn, start_state
    )
    running = attend_frames(running, keys_up, values_up, (seq_index + 1) % cycle_size * video_rows)
    running = attend_frames(
        running, keys_down, values_down, (seq_index - 1) % cycle_size * video_rows + half_rows
    )
    best_score, weight_sum, accumulated = running
    output_groups = (accumulated / jnp.maximum(weight_sum, 1.0)[:, :, None]).astype(jnp.bfloat16)
    attention_output = (
        output_groups.reshape(local_kv, GROUP, text_rows, HD)
        .transpose(2, 0, 1, 3)
        .reshape(text_rows, local_kv * GROUP * HD)
    )
    summed = lax.psum_scatter(
        lax.dot_general(
            output_weight,
            attention_output,
            (((0,), (1,)), ((), ())),
            preferred_element_type=jnp.float32,
        ).astype(jnp.bfloat16),
        "head",
        scatter_dimension=0,
        tiled=True,
    ).astype(jnp.float32)
    return (jnp.tanh(attn_gate[0]) * summed.T).astype(jnp.bfloat16)


def solution(mesh):
    in_specs = (
        P("seq", "head"),
        P(None, "head"),
        P("seq", "head"),
        P("seq", "head"),
        P("head", None),
        P(),
        P(),
        P(),
    )
    out_specs = P("seq", "head")
    return jax.shard_map(shards, mesh=mesh, in_specs=in_specs, out_specs=out_specs, check_vma=False)
```

profile of v0, /device:TPU:0, one launch (start us, length us, event | category | flops | bytes accessed | tf_op | source)
XLA Modules:
  0.0 186.2 jit_solution(13264895358251018407)
XLA Ops:
  6.5 0.7 all-gather.2.cloned.1.call-update
  7.4 0.7 copy.44
  8.3 0.7 dynamic_slice.3
  9.6 1.1 fusion.71
  10.8 46.5 %all-gather.2.cloned.1.call-done = bf16[256,4096]{1,0:T(8,128)(2,1)} async-done(((bf16[256,1024]{1,0:T(8,128)(2,1)}), bf16[256,4096]{1,0:T(8,128)(2,1)}) %all-gather.2.cloned.1.call-update) | async-done | bytes 2097168 | tf_op jit(solution)/shard_map/all_gather | solution.py:36
  57.3 6.3 %convolution_convert_fusion.1 = bf16[256,1024]{1,0:T(8,128)(2,1)S(1)} fusion(bf16[256,4096]{1,0:T(8,128)(2,1)} %all-gather.2.cloned.1.call-done, bf16[4096,1024]{1,0:T(8,128)(2,1)} %param.11), kind=kOutput, calls=%fused_computation.65 | convolution fusion | flops 2147745792 | bytes 11010048 | tf_op jit(solution)/shard_map/dot_general | solution.py:35
  64.1 59.5 %while.28 = (s32[]{:T(128)}, f32[2,1024]{1,0:T(2,128)S(1)}, f32[2,1024]{1,0:T(2,128)S(1)}, f32[2,1024,128]{2,1,0:T(8,128)S(1)}, bf16[256,256]{1,0:T(8,128)(2,1)S...) while((s32[]{:T(128)}, f32[2,1024]{1,0:T(2,128)S(1)}, ...), condition=%wide.region_8.9_spmd.clone, body=%wide.region_1.8_spmd.clone.sunk | while | flops 550279168 | bytes 23832240 | solution.py:108
  64.4 1.6 collective-permute-start.1
  66.0 1.1 collective-permute-start.2
  67.2 0.5 collective-permute-start.3
  68.2 0.6 select_reduce_fusion.6
  68.8 0.6 select_reduce_fusion.7
  69.4 0.5 fusion.116
  69.9 0.5 fusion.115
  70.4 1.2 fusion.118
  71.7 0.8 convolution_add_fusion.5
  72.6 1.2 collective-permute-start
  73.9 2.7 %collective-permute-start.2 = (bf16[256,256]{1,0:T(8,128)(2,1)S(1)}, bf16[256,256]{1,0:T(8,128)(2,1)S(1)}, u32[]{:S(2)}, u32[]{:S(2)}) collective-permute-start(bf16[256,256]{1,0:T(8,128)(2,1)S(1)} %copy.131), channel_id=1, source_target_pairs={{4,0},{8,4},{12,8},{16,12},{20,16},{24,20},{28,24},{0,28},{5,1},{9... | collective-permute-start | bytes 393224 | tf_op jit(solution)/shard_map/while/body/eval_jaxpr/ppermute | solution.py:16
  77.2 0.6 select_reduce_fusion.6
  77.7 0.6 select_reduce_fusion.7
  78.3 0.5 fusion.116
  79.4 1.2 fusion.118
  80.6 0.8 convolution_add_fusion.5
  81.5 0.8 collective-permute-start
  82.5 2.7 %collective-permute-start.2 = (bf16[256,256]{1,0:T(8,128)(2,1)S(1)}, bf16[256,256]{1,0:T(8,128)(2,1)S(1)}, u32[]{:S(2)}, u32[]{:S(2)}) collective-permute-start(bf16[256,256]{1,0:T(8,128)(2,1)S(1)} %copy.131), channel_id=1, source_target_pairs={{4,0},{8,4},{12,8},{16,12},{20,16},{24,20},{28,24},{0,28},{5,1},{9... | collective-permute-start | bytes 393224 | tf_op jit(solution)/shard_map/while/body/eval_jaxpr/ppermute | solution.py:16
  85.8 0.6 select_reduce_fusion.6
  86.3 0.6 select_reduce_fusion.7
  86.9 0.5 fusion.116
  88.0 1.2 fusion.118
  89.2 0.8 convolution_add_fusion.5
  90.7 2.7 %collective-permute-start.2 = (bf16[256,256]{1,0:T(8,128)(2,1)S(1)}, bf16[256,256]{1,0:T(8,128)(2,1)S(1)}, u32[]{:S(2)}, u32[]{:S(2)}) collective-permute-start(bf16[256,256]{1,0:T(8,128)(2,1)S(1)} %copy.131), channel_id=1, source_target_pairs={{4,0},{8,4},{12,8},{16,12},{20,16},{24,20},{28,24},{0,28},{5,1},{9... | collective-permute-start | bytes 393224 | tf_op jit(solution)/shard_map/while/body/eval_jaxpr/ppermute | solution.py:16
  94.0 0.6 select_reduce_fusion.6
  94.6 0.6 select_reduce_fusion.7
  95.2 0.5 fusion.116
  96.2 1.2 fusion.118
  97.5 0.8 convolution_add_fusion.5
  99.0 2.7 %collective-permute-start.2 = (bf16[256,256]{1,0:T(8,128)(2,1)S(1)}, bf16[256,256]{1,0:T(8,128)(2,1)S(1)}, u32[]{:S(2)}, u32[]{:S(2)}) collective-permute-start(bf16[256,256]{1,0:T(8,128)(2,1)S(1)} %copy.131), channel_id=1, source_target_pairs={{4,0},{8,4},{12,8},{16,12},{20,16},{24,20},{28,24},{0,28},{5,1},{9... | collective-permute-start | bytes 393224 | tf_op jit(solution)/shard_map/while/body/eval_jaxpr/ppermute | solution.py:16
  102.3 0.6 select_reduce_fusion.6
  102.8 0.6 select_reduce_fusion.7
  103.4 0.5 fusion.116
  104.5 1.2 fusion.118
  105.7 0.8 convolution_add_fusion.5
  106.6 0.7 collective-permute-start
  107.4 2.7 %collective-permute-start.2 = (bf16[256,256]{1,0:T(8,128)(2,1)S(1)}, bf16[256,256]{1,0:T(8,128)(2,1)S(1)}, u32[]{:S(2)}, u32[]{:S(2)}) collective-permute-start(bf16[256,256]{1,0:T(8,128)(2,1)S(1)} %copy.131), channel_id=1, source_target_pairs={{4,0},{8,4},{12,8},{16,12},{20,16},{24,20},{28,24},{0,28},{5,1},{9... | collective-permute-start | bytes 393224 | tf_op jit(solution)/shard_map/while/body/eval_jaxpr/ppermute | solution.py:16
  110.7 0.6 select_reduce_fusion.6
  111.3 0.6 select_reduce_fusion.7
  111.9 0.5 fusion.116
  112.9 1.2 fusion.118
  114.2 0.8 convolution_add_fusion.5
  115.1 0.8 collective-permute-start
  116.0 2.7 %collective-permute-start.2 = (bf16[256,256]{1,0:T(8,128)(2,1)S(1)}, bf16[256,256]{1,0:T(8,128)(2,1)S(1)}, u32[]{:S(2)}, u32[]{:S(2)}) collective-permute-start(bf16[256,256]{1,0:T(8,128)(2,1)S(1)} %copy.131), channel_id=1, source_target_pairs={{4,0},{8,4},{12,8},{16,12},{20,16},{24,20},{28,24},{0,28},{5,1},{9... | collective-permute-start | bytes 393224 | tf_op jit(solution)/shard_map/while/body/eval_jaxpr/ppermute | solution.py:16
  119.3 0.6 select_reduce_fusion.6
  119.8 0.6 select_reduce_fusion.7
  120.4 0.5 fusion.116
  121.5 1.2 fusion.118
  122.7 0.8 convolution_add_fusion.5
  123.6 0.6 select_reduce_fusion.2
  124.2 0.6 select_reduce_fusion.3
  124.8 0.5 fusion.36
  125.8 1.2 fusion.41
  127.1 1.0 fusion.42
  128.3 7.1 %fusion.35 = bf16[4096,256]{0,1:T(8,128)(2,1)} fusion(bf16[256,1024]{0,1:T(8,128)(2,1)S(1)} %bitcast.115, bf16[1024,4096]{1,0:T(8,128)(2,1)} %param.14), kind=kOutput, calls=%fused_computation.51 | convolution fusion | flops 2148532224 | bytes 11010048 | tf_op jit(solution)/shard_map/dot_general | solution.py:123
  136.1 41.3 %reduce-scatter.2.cloned.1.call-done = bf16[1024,256]{0,1:T(8,128)(2,1)} async-done(((bf16[4096,256]{0,1:T(8,128)(2,1)}), bf16[1024,256]{0,1:T(8,128)(2,1)}) %reduce-scatter.2.cloned.1.call-update) | async-done | bytes 524304 | tf_op jit(solution)/shard_map/reduce_scatter | solution.py:122
  177.4 1.9 %fusion.53 = bf16[256,1024]{1,0:T(8,128)(2,1)} fusion(bf16[1024,256]{0,1:T(8,128)(2,1)} %reduce-scatter.2.cloned.1.call-done, f32[]{:T(128)} %bitcast), kind=kLoop, calls=%fused_computation.75 | loop fusion | flops 786432 | bytes 1048580 | tf_op jit(solution)/shard_map/convert_element_type | solution.py:133
  (154 shorter events, 11.0 us)
Async XLA Ops:
  6.5 50.8 %all-gather.2.cloned.1.call-start = ((), (), s32[]{:S(2)}) async-start(), calls=%async_computation.1 | async-start | bytes 2621440 | tf_op jit(solution)/shard_map/all_gather | solution.py:36
  7.3 170.1 %reduce-scatter.2.cloned.1.call-start = ((), (), s32[]{:S(2)}) async-start(), calls=%async_computation.2 | async-start | bytes 2621440 | tf_op jit(solution)/shard_map/reduce_scatter | solution.py:122
  64.3 8.2 %collective-permute-start = (bf16[256,256]{1,0:T(8,128)(2,1)S(1)}, bf16[256,256]{1,0:T(8,128)(2,1)S(1)}, u32[]{:S(2)}, u32[]{:S(2)}) collective-permute-start(bf16[256,256]{1,0:T(8,128)(2,1)S(1)} %copy.129), channel_id=1, source_target_pairs={{28,0},{0,4},{4,8},{8,12},{12,16},{16,20},{20,24},{24,28},{29,1},{... | collective-permute-start | bytes 393224 | tf_op jit(solution)/shard_map/while/body/eval_jaxpr/ppermute | solution.py:16
  64.4 8.1 %collective-permute-start.1 = (bf16[256,256]{1,0:T(8,128)(2,1)S(1)}, bf16[256,256]{1,0:T(8,128)(2,1)S(1)}, u32[]{:S(2)}, u32[]{:S(2)}) collective-permute-start(bf16[256,256]{1,0:T(8,128)(2,1)S(1)} %copy.130), channel_id=1, source_target_pairs={{28,0},{0,4},{4,8},{8,12},{12,16},{16,20},{20,24},{24,28},{29,1},{... | collective-permute-start | bytes 393224 | tf_op jit(solution)/shard_map/while/body/eval_jaxpr/ppermute | solution.py:16
  66.0 6.5 %collective-permute-start.2 = (bf16[256,256]{1,0:T(8,128)(2,1)S(1)}, bf16[256,256]{1,0:T(8,128)(2,1)S(1)}, u32[]{:S(2)}, u32[]{:S(2)}) collective-permute-start(bf16[256,256]{1,0:T(8,128)(2,1)S(1)} %copy.131), channel_id=1, source_target_pairs={{4,0},{8,4},{12,8},{16,12},{20,16},{24,20},{28,24},{0,28},{5,1},{9... | collective-permute-start | bytes 393224 | tf_op jit(solution)/shard_map/while/body/eval_jaxpr/ppermute | solution.py:16
  67.2 5.3 %collective-permute-start.3 = (bf16[256,256]{1,0:T(8,128)(2,1)S(1)}, bf16[256,256]{1,0:T(8,128)(2,1)S(1)}, u32[]{:S(2)}, u32[]{:S(2)}) collective-permute-start(bf16[256,256]{1,0:T(8,128)(2,1)S(1)} %copy.132), channel_id=1, source_target_pairs={{4,0},{8,4},{12,8},{16,12},{20,16},{24,20},{28,24},{0,28},{5,1},{9... | collective-permute-start | bytes 393224 | tf_op jit(solution)/shard_map/while/body/eval_jaxpr/ppermute | solution.py:16
  72.6 8.9 %collective-permute-start = (bf16[256,256]{1,0:T(8,128)(2,1)S(1)}, bf16[256,256]{1,0:T(8,128)(2,1)S(1)}, u32[]{:S(2)}, u32[]{:S(2)}) collective-permute-start(bf16[256,256]{1,0:T(8,128)(2,1)S(1)} %copy.129), channel_id=1, source_target_pairs={{28,0},{0,4},{4,8},{8,12},{12,16},{16,20},{20,24},{24,28},{29,1},{... | collective-permute-start | bytes 393224 | tf_op jit(solution)/shard_map/while/body/eval_jaxpr/ppermute | solution.py:16
  73.8 7.7 %collective-permute-start.1 = (bf16[256,256]{1,0:T(8,128)(2,1)S(1)}, bf16[256,256]{1,0:T(8,128)(2,1)S(1)}, u32[]{:S(2)}, u32[]{:S(2)}) collective-permute-start(bf16[256,256]{1,0:T(8,128)(2,1)S(1)} %copy.130), channel_id=1, source_target_pairs={{28,0},{0,4},{4,8},{8,12},{12,16},{16,20},{20,24},{24,28},{29,1},{... | collective-permute-start | bytes 393224 | tf_op jit(solution)/shard_map/while/body/eval_jaxpr/ppermute | solution.py:16
  73.9 7.6 %collective-permute-start.2 = (bf16[256,256]{1,0:T(8,128)(2,1)S(1)}, bf16[256,256]{1,0:T(8,128)(2,1)S(1)}, u32[]{:S(2)}, u32[]{:S(2)}) collective-permute-start(bf16[256,256]{1,0:T(8,128)(2,1)S(1)} %copy.131), channel_id=1, source_target_pairs={{4,0},{8,4},{12,8},{16,12},{20,16},{24,20},{28,24},{0,28},{5,1},{9... | collective-permute-start | bytes 393224 | tf_op jit(solution)/shard_map/while/body/eval_jaxpr/ppermute | solution.py:16
  76.6 4.9 %collective-permute-start.3 = (bf16[256,256]{1,0:T(8,128)(2,1)S(1)}, bf16[256,256]{1,0:T(8,128)(2,1)S(1)}, u32[]{:S(2)}, u32[]{:S(2)}) collective-permute-start(bf16[256,256]{1,0:T(8,128)(2,1)S(1)} %copy.132), channel_id=1, source_target_pairs={{4,0},{8,4},{12,8},{16,12},{20,16},{24,20},{28,24},{0,28},{5,1},{9... | collective-permute-start | bytes 393224 | tf_op jit(solution)/shard_map/while/body/eval_jaxpr/ppermute | solution.py:16
  81.5 8.5 %collective-permute-start = (bf16[256,256]{1,0:T(8,128)(2,1)S(1)}, bf16[256,256]{1,0:T(8,128)(2,1)S(1)}, u32[]{:S(2)}, u32[]{:S(2)}) collective-permute-start(bf16[256,256]{1,0:T(8,128)(2,1)S(1)} %copy.129), channel_id=1, source_target_pairs={{28,0},{0,4},{4,8},{8,12},{12,16},{16,20},{20,24},{24,28},{29,1},{... | collective-permute-start | bytes 393224 | tf_op jit(solution)/shard_map/while/body/eval_jaxpr/ppermute | solution.py:16
  82.4 7.7 %collective-permute-start.1 = (bf16[256,256]{1,0:T(8,128)(2,1)S(1)}, bf16[256,256]{1,0:T(8,128)(2,1)S(1)}, u32[]{:S(2)}, u32[]{:S(2)}) collective-permute-start(bf16[256,256]{1,0:T(8,128)(2,1)S(1)} %copy.130), channel_id=1, source_target_pairs={{28,0},{0,4},{4,8},{8,12},{12,16},{16,20},{20,24},{24,28},{29,1},{... | collective-permute-start | bytes 393224 | tf_op jit(solution)/shard_map/while/body/eval_jaxpr/ppermute | solution.py:16
  82.5 7.6 %collective-permute-start.2 = (bf16[256,256]{1,0:T(8,128)(2,1)S(1)}, bf16[256,256]{1,0:T(8,128)(2,1)S(1)}, u32[]{:S(2)}, u32[]{:S(2)}) collective-permute-start(bf16[256,256]{1,0:T(8,128)(2,1)S(1)} %copy.131), channel_id=1, source_target_pairs={{4,0},{8,4},{12,8},{16,12},{20,16},{24,20},{28,24},{0,28},{5,1},{9... | collective-permute-start | bytes 393224 | tf_op jit(solution)/shard_map/while/body/eval_jaxpr/ppermute | solution.py:16
  85.1 4.9 %collective-permute-start.3 = (bf16[256,256]{1,0:T(8,128)(2,1)S(1)}, bf16[256,256]{1,0:T(8,128)(2,1)S(1)}, u32[]{:S(2)}, u32[]{:S(2)}) collective-permute-start(bf16[256,256]{1,0:T(8,128)(2,1)S(1)} %copy.132), channel_id=1, source_target_pairs={{4,0},{8,4},{12,8},{16,12},{20,16},{24,20},{28,24},{0,28},{5,1},{9... | collective-permute-start | bytes 393224 | tf_op jit(solution)/shard_map/while/body/eval_jaxpr/ppermute | solution.py:16
  90.1 8.2 %collective-permute-start = (bf16[256,256]{1,0:T(8,128)(2,1)S(1)}, bf16[256,256]{1,0:T(8,128)(2,1)S(1)}, u32[]{:S(2)}, u32[]{:S(2)}) collective-permute-start(bf16[256,256]{1,0:T(8,128)(2,1)S(1)} %copy.129), channel_id=1, source_target_pairs={{28,0},{0,4},{4,8},{8,12},{12,16},{16,20},{20,24},{24,28},{29,1},{... | collective-permute-start | bytes 393224 | tf_op jit(solution)/shard_map/while/body/eval_jaxpr/ppermute | solution.py:16
  90.6 7.7 %collective-permute-start.1 = (bf16[256,256]{1,0:T(8,128)(2,1)S(1)}, bf16[256,256]{1,0:T(8,128)(2,1)S(1)}, u32[]{:S(2)}, u32[]{:S(2)}) collective-permute-start(bf16[256,256]{1,0:T(8,128)(2,1)S(1)} %copy.130), channel_id=1, source_target_pairs={{28,0},{0,4},{4,8},{8,12},{12,16},{16,20},{20,24},{24,28},{29,1},{... | collective-permute-start | bytes 393224 | tf_op jit(solution)/shard_map/while/body/eval_jaxpr/ppermute | solution.py:16
  90.7 7.6 %collective-permute-start.2 = (bf16[256,256]{1,0:T(8,128)(2,1)S(1)}, bf16[256,256]{1,0:T(8,128)(2,1)S(1)}, u32[]{:S(2)}, u32[]{:S(2)}) collective-permute-start(bf16[256,256]{1,0:T(8,128)(2,1)S(1)} %copy.131), channel_id=1, source_target_pairs={{4,0},{8,4},{12,8},{16,12},{20,16},{24,20},{28,24},{0,28},{5,1},{9... | collective-permute-start | bytes 393224 | tf_op jit(solution)/shard_map/while/body/eval_jaxpr/ppermute | solution.py:16
  93.4 4.9 %collective-permute-start.3 = (bf16[256,256]{1,0:T(8,128)(2,1)S(1)}, bf16[256,256]{1,0:T(8,128)(2,1)S(1)}, u32[]{:S(2)}, u32[]{:S(2)}) collective-permute-start(bf16[256,256]{1,0:T(8,128)(2,1)S(1)} %copy.132), channel_id=1, source_target_pairs={{4,0},{8,4},{12,8},{16,12},{20,16},{24,20},{28,24},{0,28},{5,1},{9... | collective-permute-start | bytes 393224 | tf_op jit(solution)/shard_map/while/body/eval_jaxpr/ppermute | solution.py:16
  98.4 8.2 %collective-permute-start = (bf16[256,256]{1,0:T(8,128)(2,1)S(1)}, bf16[256,256]{1,0:T(8,128)(2,1)S(1)}, u32[]{:S(2)}, u32[]{:S(2)}) collective-permute-start(bf16[256,256]{1,0:T(8,128)(2,1)S(1)} %copy.129), channel_id=1, source_target_pairs={{28,0},{0,4},{4,8},{8,12},{12,16},{16,20},{20,24},{24,28},{29,1},{... | collective-permute-start | bytes 393224 | tf_op jit(solution)/shard_map/while/body/eval_jaxpr/ppermute | solution.py:16
  98.9 7.7 %collective-permute-start.1 = (bf16[256,256]{1,0:T(8,128)(2,1)S(1)}, bf16[256,256]{1,0:T(8,128)(2,1)S(1)}, u32[]{:S(2)}, u32[]{:S(2)}) collective-permute-start(bf16[256,256]{1,0:T(8,128)(2,1)S(1)} %copy.130), channel_id=1, source_target_pairs={{28,0},{0,4},{4,8},{8,12},{12,16},{16,20},{20,24},{24,28},{29,1},{... | collective-permute-start | bytes 393224 | tf_op jit(solution)/shard_map/while/body/eval_jaxpr/ppermute | solution.py:16
  99.0 7.6 %collective-permute-start.2 = (bf16[256,256]{1,0:T(8,128)(2,1)S(1)}, bf16[256,256]{1,0:T(8,128)(2,1)S(1)}, u32[]{:S(2)}, u32[]{:S(2)}) collective-permute-start(bf16[256,256]{1,0:T(8,128)(2,1)S(1)} %copy.131), channel_id=1, source_target_pairs={{4,0},{8,4},{12,8},{16,12},{20,16},{24,20},{28,24},{0,28},{5,1},{9... | collective-permute-start | bytes 393224 | tf_op jit(solution)/shard_map/while/body/eval_jaxpr/ppermute | solution.py:16
  101.7 4.9 %collective-permute-start.3 = (bf16[256,256]{1,0:T(8,128)(2,1)S(1)}, bf16[256,256]{1,0:T(8,128)(2,1)S(1)}, u32[]{:S(2)}, u32[]{:S(2)}) collective-permute-start(bf16[256,256]{1,0:T(8,128)(2,1)S(1)} %copy.132), channel_id=1, source_target_pairs={{4,0},{8,4},{12,8},{16,12},{20,16},{24,20},{28,24},{0,28},{5,1},{9... | collective-permute-start | bytes 393224 | tf_op jit(solution)/shard_map/while/body/eval_jaxpr/ppermute | solution.py:16
  106.6 8.4 %collective-permute-start = (bf16[256,256]{1,0:T(8,128)(2,1)S(1)}, bf16[256,256]{1,0:T(8,128)(2,1)S(1)}, u32[]{:S(2)}, u32[]{:S(2)}) collective-permute-start(bf16[256,256]{1,0:T(8,128)(2,1)S(1)} %copy.129), channel_id=1, source_target_pairs={{28,0},{0,4},{4,8},{8,12},{12,16},{16,20},{20,24},{24,28},{29,1},{... | collective-permute-start | bytes 393224 | tf_op jit(solution)/shard_map/while/body/eval_jaxpr/ppermute | solution.py:16
  107.3 7.7 %collective-permute-start.1 = (bf16[256,256]{1,0:T(8,128)(2,1)S(1)}, bf16[256,256]{1,0:T(8,128)(2,1)S(1)}, u32[]{:S(2)}, u32[]{:S(2)}) collective-permute-start(bf16[256,256]{1,0:T(8,128)(2,1)S(1)} %copy.130), channel_id=1, source_target_pairs={{28,0},{0,4},{4,8},{8,12},{12,16},{16,20},{20,24},{24,28},{29,1},{... | collective-permute-start | bytes 393224 | tf_op jit(solution)/shard_map/while/body/eval_jaxpr/ppermute | solution.py:16
  107.4 7.6 %collective-permute-start.2 = (bf16[256,256]{1,0:T(8,128)(2,1)S(1)}, bf16[256,256]{1,0:T(8,128)(2,1)S(1)}, u32[]{:S(2)}, u32[]{:S(2)}) collective-permute-start(bf16[256,256]{1,0:T(8,128)(2,1)S(1)} %copy.131), channel_id=1, source_target_pairs={{4,0},{8,4},{12,8},{16,12},{20,16},{24,20},{28,24},{0,28},{5,1},{9... | collective-permute-start | bytes 393224 | tf_op jit(solution)/shard_map/while/body/eval_jaxpr/ppermute | solution.py:16
  110.1 4.9 %collective-permute-start.3 = (bf16[256,256]{1,0:T(8,128)(2,1)S(1)}, bf16[256,256]{1,0:T(8,128)(2,1)S(1)}, u32[]{:S(2)}, u32[]{:S(2)}) collective-permute-start(bf16[256,256]{1,0:T(8,128)(2,1)S(1)} %copy.132), channel_id=1, source_target_pairs={{4,0},{8,4},{12,8},{16,12},{20,16},{24,20},{28,24},{0,28},{5,1},{9... | collective-permute-start | bytes 393224 | tf_op jit(solution)/shard_map/while/body/eval_jaxpr/ppermute | solution.py:16
  115.1 8.5 %collective-permute-start = (bf16[256,256]{1,0:T(8,128)(2,1)S(1)}, bf16[256,256]{1,0:T(8,128)(2,1)S(1)}, u32[]{:S(2)}, u32[]{:S(2)}) collective-permute-start(bf16[256,256]{1,0:T(8,128)(2,1)S(1)} %copy.129), channel_id=1, source_target_pairs={{28,0},{0,4},{4,8},{8,12},{12,16},{16,20},{20,24},{24,28},{29,1},{... | collective-permute-start | bytes 393224 | tf_op jit(solution)/shard_map/while/body/eval_jaxpr/ppermute | solution.py:16
  115.9 7.7 %collective-permute-start.1 = (bf16[256,256]{1,0:T(8,128)(2,1)S(1)}, bf16[256,256]{1,0:T(8,128)(2,1)S(1)}, u32[]{:S(2)}, u32[]{:S(2)}) collective-permute-start(bf16[256,256]{1,0:T(8,128)(2,1)S(1)} %copy.130), channel_id=1, source_target_pairs={{28,0},{0,4},{4,8},{8,12},{12,16},{16,20},{20,24},{24,28},{29,1},{... | collective-permute-start | bytes 393224 | tf_op jit(solution)/shard_map/while/body/eval_jaxpr/ppermute | solution.py:16
  116.0 7.6 %collective-permute-start.2 = (bf16[256,256]{1,0:T(8,128)(2,1)S(1)}, bf16[256,256]{1,0:T(8,128)(2,1)S(1)}, u32[]{:S(2)}, u32[]{:S(2)}) collective-permute-start(bf16[256,256]{1,0:T(8,128)(2,1)S(1)} %copy.131), channel_id=1, source_target_pairs={{4,0},{8,4},{12,8},{16,12},{20,16},{24,20},{28,24},{0,28},{5,1},{9... | collective-permute-start | bytes 393224 | tf_op jit(solution)/shard_map/while/body/eval_jaxpr/ppermute | solution.py:16
  118.7 4.9 %collective-permute-start.3 = (bf16[256,256]{1,0:T(8,128)(2,1)S(1)}, bf16[256,256]{1,0:T(8,128)(2,1)S(1)}, u32[]{:S(2)}, u32[]{:S(2)}) collective-permute-start(bf16[256,256]{1,0:T(8,128)(2,1)S(1)} %copy.132), channel_id=1, source_target_pairs={{4,0},{8,4},{12,8},{16,12},{20,16},{24,20},{28,24},{0,28},{5,1},{9... | collective-permute-start | bytes 393224 | tf_op jit(solution)/shard_map/while/body/eval_jaxpr/ppermute | solution.py:16
Sparse Core Ops, SparseCore 0:
  8.9 48.3 all-gather.1
  135.5 41.8 reduce-scatter.1
where the time goes:
time: 186 us
  waiting for transfers between devices  88.7 us (48%)
  matrix products  39.2 us (21%)
  starting transfers between devices  24.9 us (13%)
  other arithmetic  14.2 us (8%)
  between operations  14.2 us (8%)
  local copies, waits for them, and re-layouts  3.76 us (2%)
    all_gather x1, waiting for transfers between devices, shards(): lax.all_gather(text_states, 'head', axis=1, tiled=True)  46.5 us
    reduce_scatter x1, waiting for transfers between devices, shards(): lax.psum_scatter(lax.dot_general(output_weight, attention_output, (((0,),...  41.3 us
    ppermute x28, starting transfers between devices, from_behind(): return lax.ppermute(block, axis, route)  24.9 us
    dot_general x16, matrix products, dense_block(): jnp.einsum('vus,svg->vug', weights.astype(jnp.bfloat16), value_heads, pre...  16.7 us
    dot_general x16, matrix products, dense_block(): jnp.einsum('sxn,lsn->sxl', grouped_queries, key_head_count, preferred_ele...  9.04 us
    reduce_sum x16, other arithmetic, dense_block(): weight_sum = weight_sum * factor + jnp.sum(weights, axis=2)  8.05 us
    dot_general x1, matrix products, shards(): lax.dot_general(output_weight, attention_output, (((0,), (1,)), ((), ()))...  7.11 us
    dot_general x1, matrix products, shards(): jnp.dot(lax.all_gather(text_states, 'head', axis=1, tiled=True), query_we...  6.34 us
  transfers between devices with their start and end apart: 30, of which 2 were waited for; matrix products, arithmetic and copies ran while one was open for 20% of the time, Pallas kernels for 0%

commit v1 on v0

--- a/solution.py
+++ b/solution.py
@@ -33,7 +33,7 @@
     cycle_size = lax.axis_size("seq")
     score_scale = 1.0 / math.sqrt(HD)
     queries = jnp.dot(
-        lax.all_gather(text_states, "head", axis=1, tiled=True),
+        jnp.concatenate(lax.all_gather(text_states, "head"), axis=1),
         query_weight,
         preferred_element_type=jnp.float32,
     ).astype(jnp.bfloat16)

time: 186 us -> 191 us (1.027)
  local copies, waits for them, and re-layouts: 3.76 us -> 7.73 us
    reshape x0 -> x1, local copies, waits for them, and re-layouts: none -> 2.85 us  [shards(): jnp.concatenate(lax.all_gather(text_states, 'head'), axis=1)]
  transfers between devices with their start and end apart: 30 -> 30, of which waited for: 2 -> 2; matrix products, arithmetic and copies ran while one was open for 20% -> 19% of each run, Pallas kernels for 0% -> 0%
where the time goes in v1:
time: 191 us; the launch traced here: 190 us
  waiting for transfers between devices  88.5 us (46%)
  matrix products  39.3 us (21%)
  starting transfers between devices  24.9 us (13%)
  between operations  14.3 us (7%)
  other arithmetic  14.2 us (7%)
  local copies, waits for them, and re-layouts  7.73 us (4%)
    all_gather x1, waiting for transfers between devices, shards(): lax.all_gather(text_states, 'head')  46.5 us
    reduce_scatter x1, waiting for transfers between devices, shards(): lax.psum_scatter(lax.dot_general(output_weight, attention_output, (((0,),...  41.1 us
    ppermute x28, starting transfers between devices, from_behind(): return lax.ppermute(block, axis, route)  24.9 us
    dot_general x16, matrix products, dense_block(): jnp.einsum('vus,svg->vug', weights.astype(jnp.bfloat16), value_heads, pre...  16.6 us
    dot_general x16, matrix products, dense_block(): jnp.einsum('sxn,lsn->sxl', grouped_queries, key_head_count, preferred_ele...  9.08 us
    reduce_sum x16, other arithmetic, dense_block(): weight_sum = weight_sum * factor + jnp.sum(weights, axis=2)  8.05 us
    dot_general x1, matrix products, shards(): lax.dot_general(output_weight, attention_output, (((0,), (1,)), ((), ()))...  7.11 us
    dot_general x1, matrix products, shards(): jnp.dot(jnp.concatenate(lax.all_gather(text_states, 'head'), axis=1), que...  6.54 us
  transfers between devices with their start and end apart: 30, of which 2 were waited for; matrix products, arithmetic and copies ran while one was open for 19% of the time, Pallas kernels for 0%

profile of v1, /device:TPU:0, one launch (start us, length us, event | category | flops | bytes accessed | tf_op | source)
XLA Modules:
  0.0 190.1 jit_solution(11771245145162486520)
XLA Ops:
  6.5 0.7 all-gather.3.cloned.1.call-update
  7.4 0.7 copy.60
  8.3 0.7 dynamic_slice.3
  9.6 1.1 fusion.71
  10.8 46.5 %all-gather.3.cloned.1.call-done = bf16[1024,1024]{1,0:T(8,128)(2,1)} async-done(((bf16[256,1024]{1,0:T(8,128)(2,1)}), bf16[1024,1024]{1,0:T(8,128)(2,1)}) %all-gather.3.cloned.1.call-update) | async-done | bytes 2097168 | tf_op jit(solution)/shard_map/all_gather | solution.py:36
  57.3 2.8 %copy.61 = bf16[256,4,1024]{0,2,1:T(8,128)(2,1)S(1)} copy(bf16[256,4,1024]{2,0,1:T(8,128)(2,1)} %bitcast.121) | data formatting | bytes 4194304 | tf_op jit(solution)/shard_map/reshape | solution.py:36
  60.2 6.5 %convolution_convert_fusion.1 = bf16[256,1024]{1,0:T(8,128)(2,1)} fusion(bf16[256,4096]{0,1:T(8,128)(2,1)S(1)} %bitcast.119, bf16[4096,1024]{1,0:T(8,128)(2,1)} %param.11), kind=kOutput, calls=%fused_computation.65 | convolution fusion | flops 2147745792 | bytes 11010048 | tf_op jit(solution)/shard_map/dot_general | solution.py:35
  66.7 1.5 reshape.269
  68.3 59.5 %while.28 = (s32[]{:T(128)}, f32[2,1024]{1,0:T(2,128)S(1)}, f32[2,1024]{1,0:T(2,128)S(1)}, f32[2,1024,128]{2,1,0:T(8,128)S(1)}, bf16[256,256]{1,0:T(8,128)(2,1)S...) while((s32[]{:T(128)}, f32[2,1024]{1,0:T(2,128)S(1)}, ...), condition=%wide.region_8.9_spmd.clone, body=%wide.region_1.8_spmd.clone.sunk | while | flops 550279168 | bytes 23832240 | solution.py:108
  68.4 1.6 collective-permute-start.1
  70.0 1.1 collective-permute-start.2
  71.2 0.5 collective-permute-start.3
  72.2 0.6 select_reduce_fusion.6
  72.8 0.6 select_reduce_fusion.7
  73.4 0.5 fusion.116
  74.4 1.2 fusion.118
  75.7 0.8 convolution_add_fusion.5
  76.6 1.2 collective-permute-start
  77.9 2.7 %collective-permute-start.2 = (bf16[256,256]{1,0:T(8,128)(2,1)S(1)}, bf16[256,256]{1,0:T(8,128)(2,1)S(1)}, u32[]{:S(2)}, u32[]{:S(2)}) collective-permute-start(bf16[256,256]{1,0:T(8,128)(2,1)S(1)} %copy.148), channel_id=1, source_target_pairs={{4,0},{8,4},{12,8},{16,12},{20,16},{24,20},{28,24},{0,28},{5,1},{9... | collective-permute-start | bytes 393224 | tf_op jit(solution)/shard_map/while/body/eval_jaxpr/ppermute | solution.py:16
  81.2 0.6 select_reduce_fusion.6
  81.7 0.6 select_reduce_fusion.7
  82.3 0.5 fusion.116
  83.4 1.2 fusion.118
  84.6 0.8 convolution_add_fusion.5
  85.5 0.8 collective-permute-start
  86.5 2.7 %collective-permute-start.2 = (bf16[256,256]{1,0:T(8,128)(2,1)S(1)}, bf16[256,256]{1,0:T(8,128)(2,1)S(1)}, u32[]{:S(2)}, u32[]{:S(2)}) collective-permute-start(bf16[256,256]{1,0:T(8,128)(2,1)S(1)} %copy.148), channel_id=1, source_target_pairs={{4,0},{8,4},{12,8},{16,12},{20,16},{24,20},{28,24},{0,28},{5,1},{9... | collective-permute-start | bytes 393224 | tf_op jit(solution)/shard_map/while/body/eval_jaxpr/ppermute | solution.py:16
  89.7 0.6 select_reduce_fusion.6
  90.3 0.6 select_reduce_fusion.7
  90.9 0.5 fusion.116
  92.0 1.2 fusion.118
  93.2 0.8 convolution_add_fusion.5
  94.7 2.7 %collective-permute-start.2 = (bf16[256,256]{1,0:T(8,128)(2,1)S(1)}, bf16[256,256]{1,0:T(8,128)(2,1)S(1)}, u32[]{:S(2)}, u32[]{:S(2)}) collective-permute-start(bf16[256,256]{1,0:T(8,128)(2,1)S(1)} %copy.148), channel_id=1, source_target_pairs={{4,0},{8,4},{12,8},{16,12},{20,16},{24,20},{28,24},{0,28},{5,1},{9... | collective-permute-start | bytes 393224 | tf_op jit(solution)/shard_map/while/body/eval_jaxpr/ppermute | solution.py:16
  98.0 0.6 select_reduce_fusion.6
  98.6 0.6 select_reduce_fusion.7
  99.2 0.5 fusion.116
  100.2 1.2 fusion.118
  101.4 0.8 convolution_add_fusion.5
  103.0 2.7 %collective-permute-start.2 = (bf16[256,256]{1,0:T(8,128)(2,1)S(1)}, bf16[256,256]{1,0:T(8,128)(2,1)S(1)}, u32[]{:S(2)}, u32[]{:S(2)}) collective-permute-start(bf16[256,256]{1,0:T(8,128)(2,1)S(1)} %copy.148), channel_id=1, source_target_pairs={{4,0},{8,4},{12,8},{16,12},{20,16},{24,20},{28,24},{0,28},{5,1},{9... | collective-permute-start | bytes 393224 | tf_op jit(solution)/shard_map/while/body/eval_jaxpr/ppermute | solution.py:16
  106.2 0.6 select_reduce_fusion.6
  106.8 0.6 select_reduce_fusion.7
  107.4 0.5 fusion.116
  108.5 1.2 fusion.118
  109.7 0.8 convolution_add_fusion.5
  110.6 0.7 collective-permute-start
  111.4 2.7 %collective-permute-start.2 = (bf16[256,256]{1,0:T(8,128)(2,1)S(1)}, bf16[256,256]{1,0:T(8,128)(2,1)S(1)}, u32[]{:S(2)}, u32[]{:S(2)}) collective-permute-start(bf16[256,256]{1,0:T(8,128)(2,1)S(1)} %copy.148), channel_id=1, source_target_pairs={{4,0},{8,4},{12,8},{16,12},{20,16},{24,20},{28,24},{0,28},{5,1},{9... | collective-permute-start | bytes 393224 | tf_op jit(solution)/shard_map/while/body/eval_jaxpr/ppermute | solution.py:16
  114.7 0.6 select_reduce_fusion.6
  115.3 0.6 select_reduce_fusion.7
  115.9 0.5 fusion.116
  116.9 1.2 fusion.118
  118.1 0.8 convolution_add_fusion.5
  119.1 0.8 collective-permute-start
  120.0 2.7 %collective-permute-start.2 = (bf16[256,256]{1,0:T(8,128)(2,1)S(1)}, bf16[256,256]{1,0:T(8,128)(2,1)S(1)}, u32[]{:S(2)}, u32[]{:S(2)}) collective-permute-start(bf16[256,256]{1,0:T(8,128)(2,1)S(1)} %copy.148), channel_id=1, source_target_pairs={{4,0},{8,4},{12,8},{16,12},{20,16},{24,20},{28,24},{0,28},{5,1},{9... | collective-permute-start | bytes 393224 | tf_op jit(solution)/shard_map/while/body/eval_jaxpr/ppermute | solution.py:16
  123.3 0.6 select_reduce_fusion.6
  123.8 0.6 select_reduce_fusion.7
  124.4 0.5 fusion.116
  125.5 1.2 fusion.118
  126.7 0.8 convolution_add_fusion.5
  127.8 0.6 select_reduce_fusion.2
  128.4 0.6 select_reduce_fusion.3
  130.0 1.2 fusion.41
  131.2 1.0 fusion.42
  132.4 7.1 %fusion.35 = bf16[4096,256]{0,1:T(8,128)(2,1)} fusion(bf16[256,1024]{0,1:T(8,128)(2,1)S(1)} %bitcast.120, bf16[1024,4096]{1,0:T(8,128)(2,1)} %param.14), kind=kOutput, calls=%fused_computation.51 | convolution fusion | flops 2148532224 | bytes 11010048 | tf_op jit(solution)/shard_map/dot_general | solution.py:123
  140.3 41.1 %reduce-scatter.2.cloned.1.call-done = bf16[1024,256]{0,1:T(8,128)(2,1)} async-done(((bf16[4096,256]{0,1:T(8,128)(2,1)}), bf16[1024,256]{0,1:T(8,128)(2,1)}) %reduce-scatter.2.cloned.1.call-update) | async-done | bytes 524304 | tf_op jit(solution)/shard_map/reduce_scatter | solution.py:122
  181.4 1.9 %fusion.53 = bf16[256,1024]{1,0:T(8,128)(2,1)} fusion(bf16[1024,256]{0,1:T(8,128)(2,1)} %reduce-scatter.2.cloned.1.call-done, f32[]{:T(128)} %bitcast), kind=kLoop, calls=%fused_computation.75 | loop fusion | flops 786432 | bytes 1048580 | tf_op jit(solution)/shard_map/convert_element_type | solution.py:133
  (157 shorter events, 11.6 us)
Async XLA Ops:
  6.5 50.8 %all-gather.3.cloned.1.call-start = ((), (), s32[]{:S(2)}) async-start(), calls=%async_computation.2 | async-start | bytes 2621440 | tf_op jit(solution)/shard_map/all_gather | solution.py:36
  7.3 174.1 %reduce-scatter.2.cloned.1.call-start = ((), (), s32[]{:S(2)}) async-start(), calls=%async_computation.1 | async-start | bytes 2621440 | tf_op jit(solution)/shard_map/reduce_scatter | solution.py:122
  66.7 1.6 copy-start
  68.3 8.2 %collective-permute-start = (bf16[256,256]{1,0:T(8,128)(2,1)S(1)}, bf16[256,256]{1,0:T(8,128)(2,1)S(1)}, u32[]{:S(2)}, u32[]{:S(2)}) collective-permute-start(bf16[256,256]{1,0:T(8,128)(2,1)S(1)} %copy.146), channel_id=1, source_target_pairs={{28,0},{0,4},{4,8},{8,12},{12,16},{16,20},{20,24},{24,28},{29,1},{... | collective-permute-start | bytes 393224 | tf_op jit(solution)/shard_map/while/body/eval_jaxpr/ppermute | solution.py:16
  68.4 8.1 %collective-permute-start.1 = (bf16[256,256]{1,0:T(8,128)(2,1)S(1)}, bf16[256,256]{1,0:T(8,128)(2,1)S(1)}, u32[]{:S(2)}, u32[]{:S(2)}) collective-permute-start(bf16[256,256]{1,0:T(8,128)(2,1)S(1)} %copy.147), channel_id=1, source_target_pairs={{28,0},{0,4},{4,8},{8,12},{12,16},{16,20},{20,24},{24,28},{29,1},{... | collective-permute-start | bytes 393224 | tf_op jit(solution)/shard_map/while/body/eval_jaxpr/ppermute | solution.py:16
  70.0 6.5 %collective-permute-start.2 = (bf16[256,256]{1,0:T(8,128)(2,1)S(1)}, bf16[256,256]{1,0:T(8,128)(2,1)S(1)}, u32[]{:S(2)}, u32[]{:S(2)}) collective-permute-start(bf16[256,256]{1,0:T(8,128)(2,1)S(1)} %copy.148), channel_id=1, source_target_pairs={{4,0},{8,4},{12,8},{16,12},{20,16},{24,20},{28,24},{0,28},{5,1},{9... | collective-permute-start | bytes 393224 | tf_op jit(solution)/shard_map/while/body/eval_jaxpr/ppermute | solution.py:16
  71.2 5.3 %collective-permute-start.3 = (bf16[256,256]{1,0:T(8,128)(2,1)S(1)}, bf16[256,256]{1,0:T(8,128)(2,1)S(1)}, u32[]{:S(2)}, u32[]{:S(2)}) collective-permute-start(bf16[256,256]{1,0:T(8,128)(2,1)S(1)} %copy.149), channel_id=1, source_target_pairs={{4,0},{8,4},{12,8},{16,12},{20,16},{24,20},{28,24},{0,28},{5,1},{9... | collective-permute-start | bytes 393224 | tf_op jit(solution)/shard_map/while/body/eval_jaxpr/ppermute | solution.py:16
  76.6 8.9 %collective-permute-start = (bf16[256,256]{1,0:T(8,128)(2,1)S(1)}, bf16[256,256]{1,0:T(8,128)(2,1)S(1)}, u32[]{:S(2)}, u32[]{:S(2)}) collective-permute-start(bf16[256,256]{1,0:T(8,128)(2,1)S(1)} %copy.146), channel_id=1, source_target_pairs={{28,0},{0,4},{4,8},{8,12},{12,16},{16,20},{20,24},{24,28},{29,1},{... | collective-permute-start | bytes 393224 | tf_op jit(solution)/shard_map/while/body/eval_jaxpr/ppermute | solution.py:16
  77.8 7.7 %collective-permute-start.1 = (bf16[256,256]{1,0:T(8,128)(2,1)S(1)}, bf16[256,256]{1,0:T(8,128)(2,1)S(1)}, u32[]{:S(2)}, u32[]{:S(2)}) collective-permute-start(bf16[256,256]{1,0:T(8,128)(2,1)S(1)} %copy.147), channel_id=1, source_target_pairs={{28,0},{0,4},{4,8},{8,12},{12,16},{16,20},{20,24},{24,28},{29,1},{... | collective-permute-start | bytes 393224 | tf_op jit(solution)/shard_map/while/body/eval_jaxpr/ppermute | solution.py:16
  77.9 7.6 %collective-permute-start.2 = (bf16[256,256]{1,0:T(8,128)(2,1)S(1)}, bf16[256,256]{1,0:T(8,128)(2,1)S(1)}, u32[]{:S(2)}, u32[]{:S(2)}) collective-permute-start(bf16[256,256]{1,0:T(8,128)(2,1)S(1)} %copy.148), channel_id=1, source_target_pairs={{4,0},{8,4},{12,8},{16,12},{20,16},{24,20},{28,24},{0,28},{5,1},{9... | collective-permute-start | bytes 393224 | tf_op jit(solution)/shard_map/while/body/eval_jaxpr/ppermute | solution.py:16
  80.6 4.9 %collective-permute-start.3 = (bf16[256,256]{1,0:T(8,128)(2,1)S(1)}, bf16[256,256]{1,0:T(8,128)(2,1)S(1)}, u32[]{:S(2)}, u32[]{:S(2)}) collective-permute-start(bf16[256,256]{1,0:T(8,128)(2,1)S(1)} %copy.149), channel_id=1, source_target_pairs={{4,0},{8,4},{12,8},{16,12},{20,16},{24,20},{28,24},{0,28},{5,1},{9... | collective-permute-start | bytes 393224 | tf_op jit(solution)/shard_map/while/body/eval_jaxpr/ppermute | solution.py:16
  85.5 8.5 %collective-permute-start = (bf16[256,256]{1,0:T(8,128)(2,1)S(1)}, bf16[256,256]{1,0:T(8,128)(2,1)S(1)}, u32[]{:S(2)}, u32[]{:S(2)}) collective-permute-start(bf16[256,256]{1,0:T(8,128)(2,1)S(1)} %copy.146), channel_id=1, source_target_pairs={{28,0},{0,4},{4,8},{8,12},{12,16},{16,20},{20,24},{24,28},{29,1},{... | collective-permute-start | bytes 393224 | tf_op jit(solution)/shard_map/while/body/eval_jaxpr/ppermute | solution.py:16
  86.4 7.7 %collective-permute-start.1 = (bf16[256,256]{1,0:T(8,128)(2,1)S(1)}, bf16[256,256]{1,0:T(8,128)(2,1)S(1)}, u32[]{:S(2)}, u32[]{:S(2)}) collective-permute-start(bf16[256,256]{1,0:T(8,128)(2,1)S(1)} %copy.147), channel_id=1, source_target_pairs={{28,0},{0,4},{4,8},{8,12},{12,16},{16,20},{20,24},{24,28},{29,1},{... | collective-permute-start | bytes 393224 | tf_op jit(solution)/shard_map/while/body/eval_jaxpr/ppermute | solution.py:16
  86.5 7.6 %collective-permute-start.2 = (bf16[256,256]{1,0:T(8,128)(2,1)S(1)}, bf16[256,256]{1,0:T(8,128)(2,1)S(1)}, u32[]{:S(2)}, u32[]{:S(2)}) collective-permute-start(bf16[256,256]{1,0:T(8,128)(2,1)S(1)} %copy.148), channel_id=1, source_target_pairs={{4,0},{8,4},{12,8},{16,12},{20,16},{24,20},{28,24},{0,28},{5,1},{9... | collective-permute-start | bytes 393224 | tf_op jit(solution)/shard_map/while/body/eval_jaxpr/ppermute | solution.py:16
  89.1 4.9 %collective-permute-start.3 = (bf16[256,256]{1,0:T(8,128)(2,1)S(1)}, bf16[256,256]{1,0:T(8,128)(2,1)S(1)}, u32[]{:S(2)}, u32[]{:S(2)}) collective-permute-start(bf16[256,256]{1,0:T(8,128)(2,1)S(1)} %copy.149), channel_id=1, source_target_pairs={{4,0},{8,4},{12,8},{16,12},{20,16},{24,20},{28,24},{0,28},{5,1},{9... | collective-permute-start | bytes 393224 | tf_op jit(solution)/shard_map/while/body/eval_jaxpr/ppermute | solution.py:16
  94.1 8.2 %collective-permute-start = (bf16[256,256]{1,0:T(8,128)(2,1)S(1)}, bf16[256,256]{1,0:T(8,128)(2,1)S(1)}, u32[]{:S(2)}, u32[]{:S(2)}) collective-permute-start(bf16[256,256]{1,0:T(8,128)(2,1)S(1)} %copy.146), channel_id=1, source_target_pairs={{28,0},{0,4},{4,8},{8,12},{12,16},{16,20},{20,24},{24,28},{29,1},{... | collective-permute-start | bytes 393224 | tf_op jit(solution)/shard_map/while/body/eval_jaxpr/ppermute | solution.py:16
  94.6 7.7 %collective-permute-start.1 = (bf16[256,256]{1,0:T(8,128)(2,1)S(1)}, bf16[256,256]{1,0:T(8,128)(2,1)S(1)}, u32[]{:S(2)}, u32[]{:S(2)}) collective-permute-start(bf16[256,256]{1,0:T(8,128)(2,1)S(1)} %copy.147), channel_id=1, source_target_pairs={{28,0},{0,4},{4,8},{8,12},{12,16},{16,20},{20,24},{24,28},{29,1},{... | collective-permute-start | bytes 393224 | tf_op jit(solution)/shard_map/while/body/eval_jaxpr/ppermute | solution.py:16
  94.7 7.6 %collective-permute-start.2 = (bf16[256,256]{1,0:T(8,128)(2,1)S(1)}, bf16[256,256]{1,0:T(8,128)(2,1)S(1)}, u32[]{:S(2)}, u32[]{:S(2)}) collective-permute-start(bf16[256,256]{1,0:T(8,128)(2,1)S(1)} %copy.148), channel_id=1, source_target_pairs={{4,0},{8,4},{12,8},{16,12},{20,16},{24,20},{28,24},{0,28},{5,1},{9... | collective-permute-start | bytes 393224 | tf_op jit(solution)/shard_map/while/body/eval_jaxpr/ppermute | solution.py:16
  97.4 4.9 %collective-permute-start.3 = (bf16[256,256]{1,0:T(8,128)(2,1)S(1)}, bf16[256,256]{1,0:T(8,128)(2,1)S(1)}, u32[]{:S(2)}, u32[]{:S(2)}) collective-permute-start(bf16[256,256]{1,0:T(8,128)(2,1)S(1)} %copy.149), channel_id=1, source_target_pairs={{4,0},{8,4},{12,8},{16,12},{20,16},{24,20},{28,24},{0,28},{5,1},{9... | collective-permute-start | bytes 393224 | tf_op jit(solution)/shard_map/while/body/eval_jaxpr/ppermute | solution.py:16
  102.4 8.2 %collective-permute-start = (bf16[256,256]{1,0:T(8,128)(2,1)S(1)}, bf16[256,256]{1,0:T(8,128)(2,1)S(1)}, u32[]{:S(2)}, u32[]{:S(2)}) collective-permute-start(bf16[256,256]{1,0:T(8,128)(2,1)S(1)} %copy.146), channel_id=1, source_target_pairs={{28,0},{0,4},{4,8},{8,12},{12,16},{16,20},{20,24},{24,28},{29,1},{... | collective-permute-start | bytes 393224 | tf_op jit(solution)/shard_map/while/body/eval_jaxpr/ppermute | solution.py:16
  102.9 7.7 %collective-permute-start.1 = (bf16[256,256]{1,0:T(8,128)(2,1)S(1)}, bf16[256,256]{1,0:T(8,128)(2,1)S(1)}, u32[]{:S(2)}, u32[]{:S(2)}) collective-permute-start(bf16[256,256]{1,0:T(8,128)(2,1)S(1)} %copy.147), channel_id=1, source_target_pairs={{28,0},{0,4},{4,8},{8,12},{12,16},{16,20},{20,24},{24,28},{29,1},{... | collective-permute-start | bytes 393224 | tf_op jit(solution)/shard_map/while/body/eval_jaxpr/ppermute | solution.py:16
  103.0 7.6 %collective-permute-start.2 = (bf16[256,256]{1,0:T(8,128)(2,1)S(1)}, bf16[256,256]{1,0:T(8,128)(2,1)S(1)}, u32[]{:S(2)}, u32[]{:S(2)}) collective-permute-start(bf16[256,256]{1,0:T(8,128)(2,1)S(1)} %copy.148), channel_id=1, source_target_pairs={{4,0},{8,4},{12,8},{16,12},{20,16},{24,20},{28,24},{0,28},{5,1},{9... | collective-permute-start | bytes 393224 | tf_op jit(solution)/shard_map/while/body/eval_jaxpr/ppermute | solution.py:16
  105.6 4.9 %collective-permute-start.3 = (bf16[256,256]{1,0:T(8,128)(2,1)S(1)}, bf16[256,256]{1,0:T(8,128)(2,1)S(1)}, u32[]{:S(2)}, u32[]{:S(2)}) collective-permute-start(bf16[256,256]{1,0:T(8,128)(2,1)S(1)} %copy.149), channel_id=1, source_target_pairs={{4,0},{8,4},{12,8},{16,12},{20,16},{24,20},{28,24},{0,28},{5,1},{9... | collective-permute-start | bytes 393224 | tf_op jit(solution)/shard_map/while/body/eval_jaxpr/ppermute | solution.py:16
  110.6 8.4 %collective-permute-start = (bf16[256,256]{1,0:T(8,128)(2,1)S(1)}, bf16[256,256]{1,0:T(8,128)(2,1)S(1)}, u32[]{:S(2)}, u32[]{:S(2)}) collective-permute-start(bf16[256,256]{1,0:T(8,128)(2,1)S(1)} %copy.146), channel_id=1, source_target_pairs={{28,0},{0,4},{4,8},{8,12},{12,16},{16,20},{20,24},{24,28},{29,1},{... | collective-permute-start | bytes 393224 | tf_op jit(solution)/shard_map/while/body/eval_jaxpr/ppermute | solution.py:16
  111.3 7.7 %collective-permute-start.1 = (bf16[256,256]{1,0:T(8,128)(2,1)S(1)}, bf16[256,256]{1,0:T(8,128)(2,1)S(1)}, u32[]{:S(2)}, u32[]{:S(2)}) collective-permute-start(bf16[256,256]{1,0:T(8,128)(2,1)S(1)} %copy.147), channel_id=1, source_target_pairs={{28,0},{0,4},{4,8},{8,12},{12,16},{16,20},{20,24},{24,28},{29,1},{... | collective-permute-start | bytes 393224 | tf_op jit(solution)/shard_map/while/body/eval_jaxpr/ppermute | solution.py:16
  111.4 7.6 %collective-permute-start.2 = (bf16[256,256]{1,0:T(8,128)(2,1)S(1)}, bf16[256,256]{1,0:T(8,128)(2,1)S(1)}, u32[]{:S(2)}, u32[]{:S(2)}) collective-permute-start(bf16[256,256]{1,0:T(8,128)(2,1)S(1)} %copy.148), channel_id=1, source_target_pairs={{4,0},{8,4},{12,8},{16,12},{20,16},{24,20},{28,24},{0,28},{5,1},{9... | collective-permute-start | bytes 393224 | tf_op jit(solution)/shard_map/while/body/eval_jaxpr/ppermute | solution.py:16
  114.1 4.9 %collective-permute-start.3 = (bf16[256,256]{1,0:T(8,128)(2,1)S(1)}, bf16[256,256]{1,0:T(8,128)(2,1)S(1)}, u32[]{:S(2)}, u32[]{:S(2)}) collective-permute-start(bf16[256,256]{1,0:T(8,128)(2,1)S(1)} %copy.149), channel_id=1, source_target_pairs={{4,0},{8,4},{12,8},{16,12},{20,16},{24,20},{28,24},{0,28},{5,1},{9... | collective-permute-start | bytes 393224 | tf_op jit(solution)/shard_map/while/body/eval_jaxpr/ppermute | solution.py:16
  119.1 8.5 %collective-permute-start = (bf16[256,256]{1,0:T(8,128)(2,1)S(1)}, bf16[256,256]{1,0:T(8,128)(2,1)S(1)}, u32[]{:S(2)}, u32[]{:S(2)}) collective-permute-start(bf16[256,256]{1,0:T(8,128)(2,1)S(1)} %copy.146), channel_id=1, source_target_pairs={{28,0},{0,4},{4,8},{8,12},{12,16},{16,20},{20,24},{24,28},{29,1},{... | collective-permute-start | bytes 393224 | tf_op jit(solution)/shard_map/while/body/eval_jaxpr/ppermute | solution.py:16
  119.9 7.7 %collective-permute-start.1 = (bf16[256,256]{1,0:T(8,128)(2,1)S(1)}, bf16[256,256]{1,0:T(8,128)(2,1)S(1)}, u32[]{:S(2)}, u32[]{:S(2)}) collective-permute-start(bf16[256,256]{1,0:T(8,128)(2,1)S(1)} %copy.147), channel_id=1, source_target_pairs={{28,0},{0,4},{4,8},{8,12},{12,16},{16,20},{20,24},{24,28},{29,1},{... | collective-permute-start | bytes 393224 | tf_op jit(solution)/shard_map/while/body/eval_jaxpr/ppermute | solution.py:16
  120.0 7.6 %collective-permute-start.2 = (bf16[256,256]{1,0:T(8,128)(2,1)S(1)}, bf16[256,256]{1,0:T(8,128)(2,1)S(1)}, u32[]{:S(2)}, u32[]{:S(2)}) collective-permute-start(bf16[256,256]{1,0:T(8,128)(2,1)S(1)} %copy.148), channel_id=1, source_target_pairs={{4,0},{8,4},{12,8},{16,12},{20,16},{24,20},{28,24},{0,28},{5,1},{9... | collective-permute-start | bytes 393224 | tf_op jit(solution)/shard_map/while/body/eval_jaxpr/ppermute | solution.py:16
  122.7 4.9 %collective-permute-start.3 = (bf16[256,256]{1,0:T(8,128)(2,1)S(1)}, bf16[256,256]{1,0:T(8,128)(2,1)S(1)}, u32[]{:S(2)}, u32[]{:S(2)}) collective-permute-start(bf16[256,256]{1,0:T(8,128)(2,1)S(1)} %copy.149), channel_id=1, source_target_pairs={{4,0},{8,4},{12,8},{16,12},{20,16},{24,20},{28,24},{0,28},{5,1},{9... | collective-permute-start | bytes 393224 | tf_op jit(solution)/shard_map/while/body/eval_jaxpr/ppermute | solution.py:16
Sparse Core Ops, SparseCore 0:
  8.9 48.3 all-gather.2
  139.7 41.6 reduce-scatter.1
